TPU v7x, 256 devices: a whole 4x4x8 slice. The times are simulated.
256 devices in a mesh: seq: 8 (over z), chan: 32 (over y, x, core).
Axes of the slice: x: 4, y: 4, z: 8, core: 2. Of those that a mesh axis runs over, the one named last changes fastest.
Arguments:
- tokens: bfloat16 [8192, 4096], P('seq', 'chan'), may hold values from -8 to 8
- norm_gain: float32 [4096], replicated, may hold values from 0.5 to 1.5
- gate_proj: bfloat16 [4096, 8192], P(None, 'chan'), may hold values from -0.09375 to 0.09375
- inner_proj: bfloat16 [4096, 8192], P(None, 'chan'), may hold values from -0.09375 to 0.09375
- state_proj: bfloat16 [4096, 384], P('chan'), may hold values from -0.11816406 to 0.11816406
- conv_inner: float32 [4, 8192], P(None, 'chan'), may hold values from -3 to 3
- conv_state: float32 [4, 256], replicated, may hold values from -3 to 3
- log_rate: float32 [128], P('chan'), may hold values from -1 to 0
- rate_bias: float32 [128], P('chan'), may hold values from -16 to -2
- skip_gain: float32 [128], P('chan'), may hold values from 0.2 to 4
- gate_gain: float32 [8192], P('chan'), may hold values from 0.5 to 1.5
- out_proj: bfloat16 [8192, 4096], P('chan'), may hold values from -0.125 to 0.125
Outputs:
- layer_out: bfloat16 [8192, 4096], P('seq', 'chan')
All inputs are finite; a program needn't handle non-finite values.
Results may differ from a plain program's by a relative error of at most 0.012.
Values may be sent and summed in bfloat16 or wider, within the bound.
A program may use at most 128 MiB of HBM per device.

v0:
```python
import jax
import jax.numpy as jnp
from jax import lax
from jax.sharding import PartitionSpec as P

P_SIZE = 64
N = 128
K = 4
Q = 256
DI = 8192


def from_behind(value, axis, steps):
    count = lax.axis_size(axis)
    leading, last = (max(0, -steps), min(count, count - steps))
    return lax.ppermute(value, axis, [(source, source + steps) for source in range(leading, last)])


def prefix(value, axis, join, neutral):
    count, mine = (lax.axis_size(axis), lax.axis_index(axis))
    pieces = jax.tree.map(lambda part: lax.all_gather(part, axis), value)
    total = jax.tree.map(
        lambda part, zero: jnp.full_like(part, 0) + jnp.asarray(zero, part.dtype), value, neutral
    )

    def turn(position, total):
        longer = join(total, jax.tree.map(lambda part: part[position], pieces))
        return jax.tree.map(lambda new, old: jnp.where(position < mine, new, old), longer, total)

    return lax.fori_loop(0, count - 1, turn, total)


def from_everyone(x, axis):
    size = lax.axis_size(axis)
    return lax.all_to_all(jnp.broadcast_to(x[None], (size, *x.shape)), axis, 0, 0, tiled=True)


def over_copies(x, axis):
    everything = from_everyone(x, axis)
    return jnp.sum(everything, axis=0)


def causal_mix(rim_part, fresh_rows, weights):
    length = fresh_rows.shape[0]
    padded = jnp.concatenate([rim_part.astype(jnp.float32), fresh_rows.astype(jnp.float32)], axis=0)
    summed = jnp.zeros(fresh_rows.shape, jnp.float32)
    for offset in range(weights.shape[0]):
        summed = summed + weights[offset] * padded[offset : offset + length]
    return jax.nn.silu(summed)


def combine_pair(earlier_part, later_part):
    return (
        earlier_part[0] * later_part[0],
        later_part[0][:, None, None] * earlier_part[1] + later_part[1],
    )


def local(
    tokens,
    norm_gain,
    gate_proj,
    inner_proj,
    state_proj,
    conv_inner,
    conv_state,
    log_rate,
    rate_bias,
    skip_gain,
    gate_gain,
    out_proj,
):
    gathered = lax.all_gather(tokens, "chan", axis=1, tiled=True)
    widened = gathered.astype(jnp.float32)
    inverse = lax.rsqrt(jnp.mean(widened * widened, axis=1, keepdims=True) + 1e-05)
    normed = (widened * inverse * norm_gain).astype(jnp.bfloat16)
    gate_raw = jnp.dot(normed, gate_proj, preferred_element_type=jnp.float32).astype(jnp.bfloat16)
    inner_raw = jnp.dot(normed, inner_proj, preferred_element_type=jnp.float32).astype(jnp.bfloat16)
    heads = log_rate.shape[0]
    start_head = lax.axis_index("chan") * heads
    projected = jnp.dot(
        normed,
        lax.all_gather(state_proj, "chan", axis=0, tiled=True),
        preferred_element_type=jnp.float32,
    )
    state_raw = projected[:, : 2 * N]
    raw_rate = lax.dynamic_slice_in_dim(projected, 2 * N + start_head, heads, 1)
    rim_rows = from_behind(
        (inner_raw[-(K - 1) :].astype(jnp.float32), state_raw[-(K - 1) :]), "seq", 1
    )
    inner_conv = causal_mix(rim_rows[0].astype(jnp.bfloat16), inner_raw, conv_inner)
    state_conv = causal_mix(rim_rows[1], state_raw, conv_state)
    token_rows = tokens.shape[0]
    blocks = token_rows // Q
    step_size = jax.nn.softplus(raw_rate + rate_bias)
    decay_log = -jnp.exp(log_rate) * step_size
    values = inner_conv.reshape(blocks, Q, heads, P_SIZE)
    in_map = state_conv[:, :N].reshape(blocks, Q, N)
    out_map = state_conv[:, N:].reshape(blocks, Q, N)
    step_rows = step_size.reshape(blocks, Q, heads).transpose(0, 2, 1)
    log_rows = decay_log.reshape(blocks, Q, heads).transpose(0, 2, 1)
    lower_mask = (jnp.arange(Q)[:, None] >= jnp.arange(Q)[None, :]).astype(jnp.float32)
    within = jnp.einsum("chs,ts->cht", log_rows, lower_mask)
    log_gaps = within[..., :, None] - within[..., None, :]
    fading = jnp.exp(jnp.where(lower_mask > 0, log_gaps, -jnp.inf))
    scores = jnp.einsum("ctn,csn->cts", out_map, in_map)
    mixing = scores[:, None] * fading * step_rows[:, :, None, :]
    local_out = jnp.einsum("chts,cshp->cthp", mixing, values)
    tail_weight = jnp.exp(within[..., -1:] - within) * step_rows
    scaled = values * tail_weight.transpose(0, 2, 1)[..., None]
    block_end = jnp.einsum("csn,cshp->chnp", in_map, scaled)
    block_log = within[..., -1]
    through = jnp.cumsum(block_log, axis=0)
    before = through - block_log
    earlier = jnp.arange(blocks)[:, None] > jnp.arange(blocks)[None, :]
    passage = jnp.exp(
        jnp.where(earlier[:, :, None], before[:, None, :] - through[None, :, :], -jnp.inf)
    )
    entering = jnp.einsum("cdh,dhnp->chnp", passage, block_end)
    device_end = jnp.einsum("ch,chnp->hnp", jnp.exp(through[-1:] - through), block_end)
    device_fade = jnp.exp(through[-1])
    identity = (jnp.ones_like(device_fade), jnp.zeros_like(device_end))
    carried = prefix((device_fade, device_end), "seq", combine_pair, identity)[1]
    entering = entering + jnp.exp(before)[:, :, None, None] * carried[None]
    carried_out = jnp.einsum("ctn,chnp->cthp", out_map, entering)
    carried_out = carried_out * jnp.exp(within).transpose(0, 2, 1)[..., None]
    skip_wide = jnp.repeat(skip_gain, P_SIZE)
    ssd_out = (local_out + carried_out).reshape(token_rows, heads * P_SIZE) + skip_wide * inner_conv
    gated_out = ssd_out * jax.nn.silu(gate_raw.astype(jnp.float32))
    energy = over_copies(jnp.sum(gated_out * gated_out, axis=1), "chan")
    norm_scale = lax.rsqrt(energy / DI + 1e-05)
    shaped = (gated_out * norm_scale[:, None] * gate_gain).astype(jnp.bfloat16)
    column_rows = lax.all_to_all(out_proj, "chan", split_axis=1, concat_axis=0, tiled=True)
    summed = jnp.dot(
        lax.all_gather(shaped, "chan", axis=1, tiled=True),
        column_rows,
        preferred_element_type=jnp.float32,
    )
    return (tokens.astype(jnp.float32) + summed).astype(jnp.bfloat16)


def solution(mesh):
    return jax.shard_map(
        local,
        mesh=mesh,
        in_specs=(
            P("seq", "chan"),
            P(),
            P(None, "chan"),
            P(None, "chan"),
            P("chan", None),
            P(None, "chan"),
            P(),
            P("chan"),
            P("chan"),
            P("chan"),
            P("chan"),
            P("chan", None),
        ),
        out_specs=P("seq", "chan"),
        check_vma=False,
    )
```

profile of v0, /device:TPU:1, one launch (start us, length us, event | category | flops | bytes accessed | tf_op | source)
XLA Modules:
  0.0 364.0 jit_solution(8693260345117643009)
XLA Ops:
  10.4 67.4 %all-gather.7.cloned.1.call-done = bf16[1024,4096]{1,0:T(8,128)(2,1)} async-done(((bf16[1024,128]{1,0:T(8,128)(2,1)}), bf16[1024,4096]{1,0:T(8,128)(2,1)}) %all-gather.7.cloned.1.call-update) | async-done | bytes 8388624 | tf_op jit(solution)/shard_map/all_gather | solution.py:73
  77.8 5.1 %fusion.1 = f32[1024]{0:T(1024)S(1)} fusion(bf16[1024,4096]{1,0:T(8,128)(2,1)} %all-gather.7.cloned.1.call-done), kind=kLoop, calls=%fused_computation.6 | loop fusion | flops 12581888 | bytes 8392704 | tf_op jit(solution)/shard_map/reduce_sum | solution.py:75
  82.9 47.1 %all-gather.9.cloned.1.call-done = bf16[4096,384]{1,0:T(8,128)(2,1)} async-done(((bf16[128,384]{1,0:T(8,128)(2,1)}), bf16[4096,384]{1,0:T(8,128)(2,1)}) %all-gather.9.cloned.1.call-update) | async-done | bytes 3145744 | tf_op jit(solution)/shard_map/all_gather | solution.py:83
  130.0 8.1 %fusion.63 = f32[1024,384]{1,0:T(8,128)S(1)} fusion(bf16[4096,384]{1,0:T(8,128)(2,1)} %all-gather.9.cloned.1.call-done, bf16[1024,4096]{1,0:T(8,128)(2,1)} %all-gather.7.cloned.1.call-done, f32[4096]{0:T(1024)S(1)} %copy-done.10, f32[1024]{0:T(1024)S(1)} %add_rsqrt_fusion.1), kind=kOutput, calls=%fused_computation.97 | convolution fusion | flops 3238002688 | bytes 13127680 | tf_op jit(solution)/shard_map/dot_general | solution.py:81
  138.1 3.2 collective-permute-start.1
  142.3 5.9 %fusion.70 = (f32[1024,256]{1,0:T(8,128)S(1)}, bf16[1024,256]{1,0:T(8,128)(2,1)S(1)}) fusion(bf16[4096,256]{1,0:T(8,128)(2,1)S(1)} %copy-done, bf16[1024,4096]{1,0:T(8,128)(2,1)} %all-gather.7.cloned.1.call-done, f32[4096]{0:T(1024)S(1)} %copy-done.10, f32[1024]{0:T(1024)S(1)} %add_rsqrt_fusion.1), kind=kOutput, calls=%fused_computation.102 | convolution fusion | flops 2164785152 | bytes 12079104 | tf_op jit(solution)/shard_map/dot_general | solution.py:78
  148.2 3.2 collective-permute-start
  154.5 2.8 reshape.81
  158.7 3.1 divide_multiply_fusion
  164.2 12.4 %all-gather.1 = f32[8,1,4]{2,1,0:T(1,128)S(1)} all-gather(f32[1,1,4]{2,1,0:T(1,128)S(1)} %get-tuple-element.179), channel_id=1, replica_groups=mesh['seq'=8,'chan'=32] {'seq'}, dimensions={0}, use_global_device_ids=true | all-gather | bytes 144 | tf_op jit(solution)/shard_map/all_gather | solution.py:21
  176.6 2.2 fusion.71
  178.8 19.2 %all-gather.13.cloned.1.call-done = f32[32,128,64]{1,2,0:T(8,128)} async-done(((f32[4,128,64]{1,2,0:T(8,128)}), f32[32,128,64]{1,2,0:T(8,128)}) %all-gather.13.cloned.1.call-update) | async-done | bytes 1048592 | tf_op jit(solution)/shard_map/all_gather | solution.py:21
  198.0 8.4 %while.14 = (s32[]{:T(128)}, f32[4,128,64]{2,1,0:T(8,128)S(1)}, s32[]{:T(128)}, f32[8,4]{1,0:T(8,128)S(1)}, f32[8,4,128,64]{2,3,1,0:T(8,128)}, /*index=5*/s32[]{:T(128)}, s32[]{:T(128)}) while((s32[]{:T(128)}, f32[4,128,64]{2,1,0:T(8,128)S(1)}, s32[]{:T(128)}, f32[8,4]{1,0:T(8,128)S(1)}, f32[8,4,128,64]{2,3,1,0:T(8,128)}, ...), condition=%wide.region_3.4_spmd.clone, body=%wide.region_2.3_spmd.clone.sunk | while | flops 131076 | bytes 917665 | solution.py:30
  207.2 3.9 %fusion.19 = f32[4,256,4,64]{1,3,2,0:T(8,128)} fusion(f32[4,4,256]{2,1,0:T(4,128)S(1)} %copy.123, f32[4,4,256]{2,1,0:T(4,128)S(1)} %fusion.50, f32[4,256,256]{2,1,0:T(8,128)} %fusion.71, pred[256,256]{1,0:T(8,128)(4,1)S(1)} %convert_compare_fusion, f32[4,256,4,64]{1,0,3,2:T(4,128)} %reshape.81, f32[4,256,4,64]{1,3,2,0:T(8,128)S(1)} %bitcast.90, ...), kind=kOutput, calls=%fused_computation.26 | convolution fusion | flops 138936320 | bytes 4308992 | tf_op jit(solution)/shard_map/chts,cshp->cthp/dot_general | solution.py:108
  211.1 2.9 copy.152
  213.9 3.2 reshape.97
  217.2 7.8 %multiply_reduce_fusion = (f32[1024]{0:T(1024)S(1)}, f32[1024,256]{1,0:T(8,128)}) fusion(bf16[4096,256]{1,0:T(8,128)(2,1)} %param.16, bf16[1024,4096]{1,0:T(8,128)(2,1)} %all-gather.7.cloned.1.call-done, f32[4096]{0:T(1024)S(1)} %copy-done.10, f32[1024]{0:T(1024)S(1)} %add_rsqrt_fusion.1, f32[1024,256]{1,0:T(8,128)} %reshape.97, ...), kind=kOutput, calls=%fused_computation.61 | convolution fusion | flops 2167143424 | bytes 13657088 | tf_op jit(solution)/shard_map/dot_general | solution.py:77
  225.0 19.9 %all_to_all.25 = f32[32,1,1024]{2,1,0:T(1,128)S(1)} all-to-all(f32[32,1,1024]{2,1,0:T(1,128)S(1)} %broadcast_in_dim.32), channel_id=1, replica_groups=mesh['seq'=8,'chan'=32] {'chan'}, dimensions={0} | all-to-all | bytes 262144 | tf_op jit(solution)/shard_map/all_to_all | solution.py:35
  245.1 2.2 multiply_convert_fusion
  247.4 4.1 %copy.141 = bf16[256,4096]{0,1:T(8,128)(2,1)} copy(bf16[256,4096]{1,0:T(8,128)(2,1)} %param.25) | data formatting | bytes 4194304 | tf_op args[11]
  251.4 39.8 %all_to_all.26 = bf16[256,32,128]{0,2,1:T(8,128)(2,1)} all-to-all(bf16[256,32,128]{0,2,1:T(8,128)(2,1)} %bitcast.86), channel_id=1, replica_groups=mesh['seq'=8,'chan'=32] {'chan'}, dimensions={1} | all-to-all | bytes 4194304 | tf_op jit(solution)/shard_map/all_to_all | solution.py:133
  291.3 4.1 %copy.142 = bf16[32,256,128]{2,1,0:T(8,128)(2,1)} copy(bf16[32,256,128]{1,2,0:T(8,128)(2,1)} %bitcast.85) | data formatting | bytes 4194304 | tf_op jit(solution)/shard_map/all_to_all | solution.py:133
  295.3 50.5 %all-gather.11.cloned.1.call-done = bf16[1024,8192]{1,0:T(8,128)(2,1)} async-done(((bf16[1024,256]{1,0:T(8,128)(2,1)}), bf16[1024,8192]{1,0:T(8,128)(2,1)}) %all-gather.11.cloned.1.call-update) | async-done | bytes 16777232 | tf_op jit(solution)/shard_map/all_gather | solution.py:135
  345.8 11.6 %fusion.23 = bf16[1024,128]{1,0:T(8,128)(2,1)} fusion(bf16[1024,8192]{1,0:T(8,128)(2,1)} %all-gather.11.cloned.1.call-done, bf16[8192,128]{1,0:T(8,128)(2,1)} %bitcast.89, bf16[1024,128]{1,0:T(8,128)(2,1)S(1)} %copy-done.6), kind=kOutput, calls=%fused_computation.34 | convolution fusion | flops 2147876864 | bytes 19398656 | tf_op jit(solution)/shard_map/dot_general | solution.py:134
  (101 shorter events, 20.7 us)
Async XLA Ops:
  6.5 135.8 %copy-start = (bf16[4096,256]{1,0:T(8,128)(2,1)S(1)}, bf16[4096,256]{1,0:T(8,128)(2,1)}, u32[]{:S(2)}) copy-start(bf16[4096,256]{1,0:T(8,128)(2,1)} %param.17) | copy-start | bytes 6291460
  6.5 71.3 %all-gather.7.cloned.1.call-start = ((), (), s32[]{:S(2)}) async-start(), calls=%async_computation.2 | async-start | bytes 8650752 | tf_op jit(solution)/shard_map/all_gather | solution.py:73
  7.3 122.7 %all-gather.9.cloned.1.call-start = ((), (), s32[]{:S(2)}) async-start(), calls=%async_computation.3 | async-start | bytes 3244032 | tf_op jit(solution)/shard_map/all_gather | solution.py:83
  8.0 189.9 %all-gather.13.cloned.1.call-start = ((), (), s32[]{:S(2)}) async-start(), calls=%async_computation.5 | async-start | bytes 1179648 | tf_op jit(solution)/shard_map/all_gather | solution.py:21
  10.4 119.6 %copy-start.10 = (f32[4096]{0:T(1024)S(1)}, f32[4096]{0:T(1024)}, u32[]{:S(2)}) copy-start(f32[4096]{0:T(1024)} %param.15) | copy-start | bytes 49156
  82.9 58.8 %copy-start.8 = (f32[4]{0:T(128)S(1)}, f32[4]{0:T(128)}, u32[]{:S(2)}) copy-start(f32[4]{0:T(128)} %param.22) | copy-start | bytes 52
  138.1 3.2 copy-start.3
  138.1 20.6 %collective-permute-start.1 = (f32[3,256]{1,0:T(4,128)S(1)}, f32[3,256]{1,0:T(4,128)S(1)}, u32[]{:S(2)}, u32[]{:S(2)}) collective-permute-start(f32[3,256]{1,0:T(4,128)S(1)} %slice.92), channel_id=1, source_target_pairs={{0,32},{32,64},{64,96},{96,128},{128,160},{160,192},{192,224},{1,3... | collective-permute-start | bytes 9224 | tf_op jit(solution)/shard_map/ppermute | solution.py:16
  142.3 9.1 %copy-start.4 = (f32[1024,384]{1,0:T(8,128)S(1)}, f32[1024,384]{1,0:T(8,128)}, u32[]{:S(2)}) copy-start(f32[1024,384]{1,0:T(8,128)} %copy-done.3) | copy-start | bytes 4718596
  148.2 4.3 %collective-permute-start = (bf16[3,256]{1,0:T(4,128)(2,1)S(1)}, bf16[3,256]{1,0:T(4,128)(2,1)S(1)}, u32[]{:S(2)}, u32[]{:S(2)}) collective-permute-start(bf16[3,256]{1,0:T(4,128)(2,1)S(1)} %slice.161), channel_id=1, source_target_pairs={{0,32},{32,64},{64,96},{96,128},{128,160},{160,192},{192,224},{1,3... | collective-permute-start | bytes 4616 | tf_op jit(solution)/shard_map/ppermute | solution.py:16
  153.2 8.7 %copy-start.1 = (f32[1024,256]{1,0:T(8,128)}, f32[1024,256]{1,0:T(8,128)S(1)}, u32[]{:S(2)}) copy-start(f32[1024,256]{1,0:T(8,128)S(1)} %divide_multiply_fusion.1) | copy-start | bytes 3145732
  154.5 9.1 %copy-start.9 = (f32[4]{0:T(128)S(1)}, f32[4]{0:T(128)}, u32[]{:S(2)}) copy-start(f32[4]{0:T(128)} %param.23) | copy-start | bytes 52
  161.9 0.7 copy-start.5
  163.6 182.2 %all-gather.11.cloned.1.call-start = ((), (), s32[]{:S(2)}) async-start(), calls=%async_computation.4 | async-start | bytes 17301504 | tf_op jit(solution)/shard_map/all_gather | solution.py:135
  211.1 6.1 %copy-start.2 = (f32[1024,256]{1,0:T(8,128)S(1)}, f32[1024,256]{1,0:T(8,128)}, u32[]{:S(2)}) copy-start(f32[1024,256]{1,0:T(8,128)} %copy-done.1) | copy-start | bytes 3145732
  217.2 27.9 %copy-start.7 = (f32[256]{0:T(256)S(1)}, f32[256]{0:T(256)}, u32[]{:S(2)}) copy-start(f32[256]{0:T(256)} %param.24) | copy-start | bytes 3076
  251.4 94.4 %copy-start.6 = (bf16[1024,128]{1,0:T(8,128)(2,1)S(1)}, bf16[1024,128]{1,0:T(8,128)(2,1)}, u32[]{:S(2)}) copy-start(bf16[1024,128]{1,0:T(8,128)(2,1)} %param.14) | copy-start | bytes 786436
Sparse Core Ops, SparseCore 0:
  9.8 67.9 all-gather.6
  80.4 49.5 all-gather.8
  163.7 34.1 all-gather.12
  247.5 98.2 all-gather.10
where the time goes:
time: 365 us; the launch traced here: 364 us
  waiting for transfers between devices  186 us (51%)
  blocking collectives  72.1 us (20%)
  matrix products  41.3 us (11%)
  local copies, waits for them, and re-layouts  30.5 us (8%)
  other arithmetic  14.3 us (4%)
  between operations  13.4 us (4%)
  starting transfers between devices  6.52 us (2%)
    all_gather x1, waiting for transfers between devices, local(): gathered = lax.all_gather(tokens, 'chan', axis=1, tiled=True)  67.4 us
    all_gather x1, waiting for transfers between devices, local(): lax.all_gather(shaped, 'chan', axis=1, tiled=True)  50.5 us
    all_gather x1, waiting for transfers between devices, local(): lax.all_gather(state_proj, 'chan', axis=0, tiled=True)  47.1 us
    all_to_all x1, blocking collectives, local(): lax.all_to_all(out_proj, 'chan', split_axis=1, concat_axis=0, tiled=True)  39.8 us
    all_to_all x1, blocking collectives, from_everyone(): lax.all_to_all(jnp.broadcast_to(x[None], (size, *x.shape)), axis, 0, 0, t...  19.9 us
    all_gather x1, waiting for transfers between devices, prefix(): pieces = jax.tree.map(lambda part: lax.all_gather(part, axis), value)  19.2 us
    all_gather x1, blocking collectives, prefix(): pieces = jax.tree.map(lambda part: lax.all_gather(part, axis), value)  12.4 us
    dot_general x1, matrix products, local(): jnp.dot(lax.all_gather(shaped, 'chan', axis=1, tiled=True), column_rows,...  11.6 us
  transfers between devices with their start and end apart: 6, of which 4 were waited for; matrix products, arithmetic and copies ran while one was open for 9% of the time, Pallas kernels for 0%

commit v1 on v0

--- a/solution.py
+++ b/solution.py
@@ -70,7 +70,7 @@
     gate_gain,
     out_proj,
 ):
-    gathered = lax.all_gather(tokens, "chan", axis=1, tiled=True)
+    gathered = jnp.concatenate(lax.all_gather(tokens, "chan"), axis=1)
     widened = gathered.astype(jnp.float32)
     inverse = lax.rsqrt(jnp.mean(widened * widened, axis=1, keepdims=True) + 1e-05)
     normed = (widened * inverse * norm_gain).astype(jnp.bfloat16)

time: 365 us -> 349 us (0.956)
  waiting for transfers between devices: 186 us -> 144 us
  other arithmetic: 14.3 us -> 31 us
  local copies, waits for them, and re-layouts: 30.5 us -> 40.3 us
    all_gather x1, waiting for transfers between devices: 47.1 us -> 9.05 us  [local(): lax.all_gather(state_proj, 'chan', axis=0, tiled=True)]
    convert_element_type x0 -> x2, other arithmetic: none -> 20.4 us  [the longest x1 11.1 us: local(): widened = gathered.astype(jnp.float32)]
    convert_element_type x0 -> x1, local copies, waits for them, and re-layouts: none -> 17.5 us  [local(): widened = gathered.astype(jnp.float32)]
    all_gather x1, waiting for transfers between devices: 67.4 us -> 61.5 us  [local(): gathered = jnp.concatenate(lax.all_gather(tokens, 'chan'), axis=1)]
  transfers between devices with their start and end apart: 6 -> 6, of which waited for: 4 -> 5; matrix products, arithmetic and copies ran while one was open for 9% -> 18% of each run, Pallas kernels for 0% -> 0%
where the time goes in v1:
time: 349 us
  waiting for transfers between devices  144 us (41%)
  blocking collectives  73.7 us (21%)
  local copies, waits for them, and re-layouts  40.3 us (12%)
  matrix products  39.8 us (11%)
  other arithmetic  31 us (9%)
  between operations  13.4 us (4%)
  starting transfers between devices  6.48 us (2%)
    all_gather x1, waiting for transfers between devices, local(): gathered = jnp.concatenate(lax.all_gather(tokens, 'chan'), axis=1)  61.5 us
    all_gather x1, waiting for transfers between devices, local(): lax.all_gather(shaped, 'chan', axis=1, tiled=True)  50.9 us
    all_to_all x1, blocking collectives, local(): lax.all_to_all(out_proj, 'chan', split_axis=1, concat_axis=0, tiled=True)  41 us
    all_gather x1, waiting for transfers between devices, prefix(): pieces = jax.tree.map(lambda part: lax.all_gather(part, axis), value)  20.1 us
    all_to_all x1, blocking collectives, from_everyone(): lax.all_to_all(jnp.broadcast_to(x[None], (size, *x.shape)), axis, 0, 0, t...  19.9 us
    convert_element_type x1, local copies, waits for them, and re-layouts, local(): widened = gathered.astype(jnp.float32)  17.5 us
    all_gather x1, blocking collectives, prefix(): pieces = jax.tree.map(lambda part: lax.all_gather(part, axis), value)  12.8 us
    dot_general x1, matrix products, local(): jnp.dot(lax.all_gather(shaped, 'chan', axis=1, tiled=True), column_rows,...  11.8 us
  transfers between devices with their start and end apart: 6, of which 5 were waited for; matrix products, arithmetic and copies ran while one was open for 18% of the time, Pallas kernels for 0%

profile of v1, /device:TPU:1, one launch (start us, length us, event | category | flops | bytes accessed | tf_op | source)
XLA Modules:
  0.0 348.5 jit_solution(4467841990259172250)
XLA Ops:
  10.4 61.5 %all-gather.12.cloned.1.call-done = bf16[32768,128]{1,0:T(8,128)(2,1)} async-done(((bf16[1024,128]{1,0:T(8,128)(2,1)}), bf16[32768,128]{1,0:T(8,128)(2,1)}) %all-gather.12.cloned.1.call-update) | async-done | bytes 8388624 | tf_op jit(solution)/shard_map/all_gather | solution.py:73
  71.9 11.1 %convert_bitcast_fusion = f32[1024,32,128]{2,0,1:T(8,128)} fusion(bf16[32768,128]{1,0:T(8,128)(2,1)} %all-gather.12.cloned.1.call-done), kind=kLoop, calls=%fused_computation.5 | loop fusion | flops 4194304 | bytes 25165824 | tf_op jit(solution)/shard_map/convert_element_type | solution.py:74
  83.0 17.5 %copy.124 = f32[1024,32,128]{0,2,1:T(8,128)} copy(f32[1024,32,128]{2,0,1:T(8,128)} %convert_bitcast_fusion) | data formatting | bytes 33554432 | tf_op jit(solution)/shard_map/convert_element_type | solution.py:74
  100.5 5.1 %fusion.1 = f32[1024]{0:T(1024)S(1)} fusion(bf16[32,1024,128]{2,1,0:T(8,128)(2,1)} %bitcast.99), kind=kLoop, calls=%fused_computation.6 | loop fusion | flops 12581888 | bytes 8392704 | tf_op jit(solution)/shard_map/reduce_sum | solution.py:75
  105.6 9.3 %fusion.3 = bf16[1024,4096]{0,1:T(8,128)(2,1)} fusion(f32[1024,32,128]{0,2,1:T(8,128)} %copy.124, f32[4096]{0:T(1024)S(1)} %copy-done.5, f32[1024]{0:T(1024)S(1)} %add_rsqrt_fusion.1), kind=kLoop, calls=%fused_computation.9 | loop fusion | flops 12582912 | bytes 25186304 | tf_op jit(solution)/shard_map/convert_element_type | solution.py:76
  114.9 9.0 %all-gather.8.cloned.1.call-done = bf16[4096,384]{1,0:T(8,128)(2,1)} async-done(((bf16[128,384]{1,0:T(8,128)(2,1)}), bf16[4096,384]{1,0:T(8,128)(2,1)}) %all-gather.8.cloned.1.call-update) | async-done | bytes 3145744 | tf_op jit(solution)/shard_map/all_gather | solution.py:83
  123.9 7.9 %fusion.67 = f32[1024,384]{1,0:T(8,128)S(1)} fusion(bf16[1024,4096]{0,1:T(8,128)(2,1)} %fusion.3, bf16[4096,384]{1,0:T(8,128)(2,1)} %all-gather.8.cloned.1.call-done), kind=kOutput, calls=%fused_computation.103 | convolution fusion | flops 3221225472 | bytes 13107200 | tf_op jit(solution)/shard_map/dot_general | solution.py:81
  131.9 3.2 collective-permute-start.1
  136.1 5.7 %fusion.66 = (f32[1024,256]{1,0:T(8,128)S(1)}, bf16[1024,256]{1,0:T(8,128)(2,1)S(1)}) fusion(bf16[1024,4096]{0,1:T(8,128)(2,1)} %fusion.3, bf16[4096,256]{1,0:T(8,128)(2,1)S(1)} %copy-done), kind=kOutput, calls=%fused_computation.102 | convolution fusion | flops 2148007936 | bytes 12058624 | tf_op jit(solution)/shard_map/dot_general | solution.py:78
  141.8 3.2 collective-permute-start
  151.9 12.8 %all-gather.2 = f32[8,1,4]{2,1,0:T(1,128)S(1)} all-gather(f32[1,1,4]{2,1,0:T(1,128)S(1)} %get-tuple-element.179), channel_id=1, replica_groups=mesh['seq'=8,'chan'=32] {'seq'}, dimensions={0}, use_global_device_ids=true | all-gather | bytes 144 | tf_op jit(solution)/shard_map/all_gather | solution.py:21
  166.0 20.1 %all-gather.14.cloned.1.call-done = f32[32,128,64]{1,2,0:T(8,128)} async-done(((f32[4,128,64]{1,2,0:T(8,128)}), f32[32,128,64]{1,2,0:T(8,128)}) %all-gather.14.cloned.1.call-update) | async-done | bytes 1048592 | tf_op jit(solution)/shard_map/all_gather | solution.py:21
  186.1 8.4 %while.14 = (s32[]{:T(128)}, f32[4,128,64]{2,1,0:T(8,128)S(1)}, s32[]{:T(128)}, f32[8,4]{1,0:T(8,128)S(1)}, f32[8,4,128,64]{2,3,1,0:T(8,128)}, /*index=5*/s32[]{:T(128)}, s32[]{:T(128)}) while((s32[]{:T(128)}, f32[4,128,64]{2,1,0:T(8,128)S(1)}, s32[]{:T(128)}, f32[8,4]{1,0:T(8,128)S(1)}, f32[8,4,128,64]{2,3,1,0:T(8,128)}, ...), condition=%wide.region_3.4_spmd.clone, body=%wide.region_2.3_spmd.clone.sunk | while | flops 131076 | bytes 917665 | solution.py:30
  195.3 3.4 fusion.19
  198.7 1.8 copy.157
  200.6 2.1 reshape.105
  202.7 7.9 %multiply_reduce_fusion = (f32[1024]{0:T(1024)S(1)}, f32[1024,256]{1,0:T(8,128)}) fusion(bf16[1024,4096]{0,1:T(8,128)(2,1)} %fusion.3, bf16[4096,256]{1,0:T(8,128)(2,1)} %param.16, f32[1024,256]{1,0:T(8,128)} %reshape.105, f32[1024,256]{1,0:T(8,128)S(1)} %divide_multiply_fusion.1, f32[256]{0:T(256)S(1)} %mul.273), kind=kOutput, calls=%fused_computation.62 | convolution fusion | flops 2150366208 | bytes 13636608 | tf_op jit(solution)/shard_map/dot_general | solution.py:77
  210.7 19.9 %all_to_all.25 = f32[32,1,1024]{2,1,0:T(1,128)S(1)} all-to-all(f32[32,1,1024]{2,1,0:T(1,128)S(1)} %broadcast_in_dim.32), channel_id=1, replica_groups=mesh['seq'=8,'chan'=32] {'chan'}, dimensions={0} | all-to-all | bytes 262144 | tf_op jit(solution)/shard_map/all_to_all | solution.py:35
  230.7 2.2 multiply_convert_fusion
  233.0 2.5 copy.146
  235.5 41.0 %all_to_all.26 = bf16[256,32,128]{0,2,1:T(8,128)(2,1)S(1)} all-to-all(bf16[256,32,128]{0,2,1:T(8,128)(2,1)} %bitcast.101), channel_id=1, replica_groups=mesh['seq'=8,'chan'=32] {'chan'}, dimensions={1} | all-to-all | bytes 4194304 | tf_op jit(solution)/shard_map/all_to_all | solution.py:133
  276.5 2.9 copy.147
  279.4 50.9 %all-gather.10.cloned.1.call-done = bf16[1024,8192]{1,0:T(8,128)(2,1)} async-done(((bf16[1024,256]{1,0:T(8,128)(2,1)}), bf16[1024,8192]{1,0:T(8,128)(2,1)}) %all-gather.10.cloned.1.call-update) | async-done | bytes 16777232 | tf_op jit(solution)/shard_map/all_gather | solution.py:135
  330.2 11.8 %fusion.23 = bf16[1024,128]{1,0:T(8,128)(2,1)} fusion(bf16[1024,8192]{1,0:T(8,128)(2,1)} %all-gather.10.cloned.1.call-done, bf16[8192,128]{1,0:T(8,128)(2,1)} %bitcast.104, bf16[1024,128]{1,0:T(8,128)(2,1)S(1)} %copy-done.4), kind=kOutput, calls=%fused_computation.35 | convolution fusion | flops 2147876864 | bytes 19398656 | tf_op jit(solution)/shard_map/dot_general | solution.py:134
  (101 shorter events, 22.0 us)
Async XLA Ops:
  6.5 129.5 %copy-start = (bf16[4096,256]{1,0:T(8,128)(2,1)S(1)}, bf16[4096,256]{1,0:T(8,128)(2,1)}, u32[]{:S(2)}) copy-start(bf16[4096,256]{1,0:T(8,128)(2,1)} %param.17) | copy-start | bytes 6291460
  6.5 65.4 %all-gather.12.cloned.1.call-start = ((), (), s32[]{:S(2)}) async-start(), calls=%async_computation.4 | async-start | bytes 8650752 | tf_op jit(solution)/shard_map/all_gather | solution.py:73
  7.3 116.7 %all-gather.8.cloned.1.call-start = ((), (), s32[]{:S(2)}) async-start(), calls=%async_computation.2 | async-start | bytes 3244032 | tf_op jit(solution)/shard_map/all_gather | solution.py:83
  8.0 178.1 %all-gather.14.cloned.1.call-start = ((), (), s32[]{:S(2)}) async-start(), calls=%async_computation.5 | async-start | bytes 1179648 | tf_op jit(solution)/shard_map/all_gather | solution.py:21
  100.5 5.1 %copy-start.5 = (f32[4096]{0:T(1024)S(1)}, f32[4096]{0:T(1024)}, u32[]{:S(2)}) copy-start(f32[4096]{0:T(1024)} %param.15) | copy-start | bytes 49156
  114.9 20.6 %copy-start.7 = (f32[4]{0:T(128)S(1)}, f32[4]{0:T(128)}, u32[]{:S(2)}) copy-start(f32[4]{0:T(128)} %param.22) | copy-start | bytes 52
  131.9 3.2 copy-start.2
  131.9 17.8 %collective-permute-start.1 = (f32[3,256]{1,0:T(4,128)S(1)}, f32[3,256]{1,0:T(4,128)S(1)}, u32[]{:S(2)}, u32[]{:S(2)}) collective-permute-start(f32[3,256]{1,0:T(4,128)S(1)} %slice.92), channel_id=1, source_target_pairs={{0,32},{32,64},{64,96},{96,128},{128,160},{160,192},{192,224},{1,3... | collective-permute-start | bytes 9224 | tf_op jit(solution)/shard_map/ppermute | solution.py:16
  141.8 3.9 %collective-permute-start = (bf16[3,256]{1,0:T(4,128)(2,1)S(1)}, bf16[3,256]{1,0:T(4,128)(2,1)S(1)}, u32[]{:S(2)}, u32[]{:S(2)}) collective-permute-start(bf16[3,256]{1,0:T(4,128)(2,1)S(1)} %slice.161), channel_id=1, source_target_pairs={{0,32},{32,64},{64,96},{96,128},{128,160},{160,192},{192,224},{1,3... | collective-permute-start | bytes 4616 | tf_op jit(solution)/shard_map/ppermute | solution.py:16
  145.0 4.6 %slice-start = ((f32[1024,384]{1,0:T(8,128)}), f32[1024,256]{1,0:T(8,128)S(1)}, s32[]{:S(2)}) async-start(f32[1024,384]{1,0:T(8,128)} %copy-done.2), calls=%async_computation.6 | async-start | bytes 2097152 | tf_op jit(solution)/shard_map/slice | solution.py:86
  147.7 3.7 %copy-start.8 = (f32[4]{0:T(128)S(1)}, f32[4]{0:T(128)}, u32[]{:S(2)}) copy-start(f32[4]{0:T(128)} %param.23) | copy-start | bytes 52
  151.3 178.9 %all-gather.10.cloned.1.call-start = ((), (), s32[]{:S(2)}) async-start(), calls=%async_computation.3 | async-start | bytes 17301504 | tf_op jit(solution)/shard_map/all_gather | solution.py:135
  202.7 28.0 %copy-start.6 = (f32[256]{0:T(256)S(1)}, f32[256]{0:T(256)}, u32[]{:S(2)}) copy-start(f32[256]{0:T(256)} %param.24) | copy-start | bytes 3076
  202.7 30.3 %copy-start.3 = (bf16[256,4096]{1,0:T(8,128)(2,1)S(1)}, bf16[256,4096]{1,0:T(8,128)(2,1)}, u32[]{:S(2)}) copy-start(bf16[256,4096]{1,0:T(8,128)(2,1)} %param.25) | copy-start | bytes 6291460
  235.5 94.8 %copy-start.4 = (bf16[1024,128]{1,0:T(8,128)(2,1)S(1)}, bf16[1024,128]{1,0:T(8,128)(2,1)}, u32[]{:S(2)}) copy-start(bf16[1024,128]{1,0:T(8,128)(2,1)} %param.14) | copy-start | bytes 786436
  330.2 11.8 %copy-start.1 = (bf16[4096,256]{1,0:T(8,128)(2,1)S(1)}, bf16[4096,256]{1,0:T(8,128)(2,1)}, u32[]{:S(2)}) copy-start(bf16[4096,256]{1,0:T(8,128)(2,1)} %param.17) | copy-start | bytes 6291460
Sparse Core Ops, SparseCore 0:
  9.9 61.9 all-gather.11
  74.4 49.4 all-gather.7
  151.4 34.5 all-gather.13
  233.1 97.0 all-gather.9
